TPU v7x, 32 devices: a whole 2x2x4 slice. The times are simulated.
32 devices in a mesh: dom: 8 (over z, y), slab: 4 (over x, core).
Axes of the slice: x: 2, y: 2, z: 4, core: 2. Of those that a mesh axis runs over, the one named last changes fastest.
Arguments:
- particles: bfloat16 [1536, 32, 1024], P('dom', 'slab'), may hold values from -6 to 6
- refs: bfloat16 [2048, 32, 2048], P('dom', 'slab'), may hold values from -6 to 6
- orient: int32 [1536], P('dom'), may hold values from 0 to 2047, as said below
- shifts: int32 [1536, 8, 2], P('dom'), may hold values from -4 to 4
- tilt: int32 [1536], P('dom'), may hold values from 0 to 15
- wedge: float32 [16, 32, 1024], P(None, 'slab'), may hold values from 0.1 to 1
Outputs:
- new_refs: float32 [2048, 32, 2048], P('dom', 'slab')
- shift_weights: float32 [1536, 8], P('dom')
Inputs may be any that keep to these rules, and one draw needn't show every extreme that they name: `orient`: split the particles into aligned blocks of 192 (the rows of one device) and the orientations into ranges of 256. In every block at most 48 particles have orientations in any one range, and in every draw one range holds exactly 48 particles of every block.
All inputs are finite; a program needn't handle non-finite values.
Results may differ from a plain program's by a relative error of at most 0.004.
Values may be sent and summed in bfloat16 or wider, within the bound.
A program may use at most 128 MiB of HBM per device.

v0:
```python
import math
import jax
import jax.numpy as jnp
from jax import lax
from jax.sharding import PartitionSpec as P

BOX = 32
TILTS = 16
HIGH = lax.Precision.HIGHEST


def dft_table(box):
    pixel = jnp.arange(box * box, dtype=jnp.int32)
    row_y = pixel // box
    row_x = pixel % box
    phase = (row_y[:, None] * row_y[None, :] + row_x[:, None] * row_x[None, :]) % box
    angle = phase.astype(jnp.float32) * (2.0 * math.pi / box)
    return jnp.concatenate([jnp.cos(angle), -jnp.sin(angle)], axis=1).astype(jnp.bfloat16)


def factors(box):
    values = jnp.arange(-4, 5, dtype=jnp.int32)
    freq = jnp.arange(box, dtype=jnp.int32)
    phase = values[:, None] * freq[None, :] % box
    angle = phase.astype(jnp.float32) * (2.0 * math.pi / box)
    return (jnp.cos(angle), jnp.sin(angle))


def shift_bins(shifts):
    bins = (shifts[:, :, 0] + 4) * 9 + (shifts[:, :, 1] + 4)
    return (bins[:, :, None] == jnp.arange(81, dtype=jnp.int32)[None, None, :]).astype(jnp.float32)


def evaluate(cross, bins_hot, box):
    volume = box * box
    rows = cross.shape[0]
    cross_re = cross[:, :volume].reshape(rows, box, box)
    cross_im = cross[:, volume:].reshape(rows, box, box)
    cosine, sine = factors(box)
    inner_re = jnp.einsum("pyx,tx->pyt", cross_re, cosine, precision=HIGH) - jnp.einsum(
        "pyx,tx->pyt", cross_im, sine, precision=HIGH
    )
    inner_im = jnp.einsum("pyx,tx->pyt", cross_re, sine, precision=HIGH) + jnp.einsum(
        "pyx,tx->pyt", cross_im, cosine, precision=HIGH
    )
    outer_re = jnp.einsum("pyt,sy->pst", inner_re, cosine, precision=HIGH) - jnp.einsum(
        "pyt,sy->pst", inner_im, sine, precision=HIGH
    )
    every = outer_re.reshape(rows, 81)
    return jnp.einsum("pcb,pb->pc", bins_hot, every, precision=HIGH) / volume


def steer(weights, bins_hot, box):
    rows = weights.shape[0]
    cosine, sine = factors(box)
    binned = jnp.einsum("pc,pcb->pb", weights, bins_hot, precision=HIGH).reshape(rows, 9, 9)
    half_re = jnp.einsum("pst,tx->psx", binned, cosine, precision=HIGH)
    half_im = jnp.einsum("pst,tx->psx", binned, sine, precision=HIGH)
    phi_re = jnp.einsum("psx,sy->pyx", half_re, cosine, precision=HIGH) - jnp.einsum(
        "psx,sy->pyx", half_im, sine, precision=HIGH
    )
    phi_im = jnp.einsum("psx,sy->pyx", half_re, sine, precision=HIGH) + jnp.einsum(
        "psx,sy->pyx", half_im, cosine, precision=HIGH
    )
    return (phi_re.reshape(rows, box * box), phi_im.reshape(rows, box * box))


def shards(particles, refs, orient, shifts, tilt, wedge):
    count = particles.shape[0]
    planes = particles.shape[1]
    volume = particles.shape[2]
    owned = refs.shape[0]
    ncand = shifts.shape[1]
    peers = lax.axis_size("dom")
    capacity = 2 * count // peers
    slots_all = peers * capacity
    owner = orient // owned
    local = orient % owned
    owner_hot = (owner[:, None] == jnp.arange(peers, dtype=jnp.int32)[None, :]).astype(jnp.int32)
    before = jnp.cumsum(owner_hot, axis=0) - owner_hot
    rank = jnp.sum(before * owner_hot, axis=1)
    slot = owner * capacity + rank
    holder = (
        jnp.full((slots_all,), count, jnp.int32).at[slot].set(jnp.arange(count, dtype=jnp.int32))
    )
    meta = jnp.concatenate(
        [local[:, None], tilt[:, None], shifts.reshape(count, 2 * ncand)], axis=1
    )
    out_rows = jnp.take(particles, holder, axis=0, mode="fill", fill_value=0).reshape(
        peers, capacity, planes, volume
    )
    out_meta = jnp.take(meta, holder, axis=0, mode="fill", fill_value=-1).reshape(
        peers, capacity, 2 * ncand + 2
    )
    in_rows, in_meta = (
        lax.all_to_all(out_rows, "dom", split_axis=0, concat_axis=0, tiled=True),
        lax.all_to_all(out_meta, "dom", split_axis=0, concat_axis=0, tiled=True),
    )
    in_meta = in_meta.reshape(slots_all, 2 * ncand + 2)
    asked_local = in_meta[:, 0]
    safe = jnp.where(asked_local < 0, owned, asked_local)
    fetched = jnp.take(refs, safe, axis=0, mode="fill", fill_value=0)
    work_rows = in_rows.reshape(slots_all, planes, volume)
    work_shifts = in_meta[:, 2:].reshape(slots_all, ncand, 2)
    work_tilt = in_meta[:, 1]
    rows_here = work_rows.shape[0]
    bins_hot = shift_bins(work_shifts)
    table = dft_table(BOX)
    spectrum = jnp.dot(
        work_rows.reshape(rows_here * planes, volume), table, preferred_element_type=jnp.float32
    ).reshape(rows_here, planes, 2 * volume)
    spec_re = spectrum[:, :, :volume]
    spec_im = spectrum[:, :, volume:]
    ref_re = fetched[:, :, :volume].astype(jnp.float32)
    ref_im = fetched[:, :, volume:].astype(jnp.float32)
    cross = jnp.concatenate(
        [
            jnp.sum(spec_re * ref_re + spec_im * ref_im, axis=1),
            jnp.sum(spec_im * ref_re - spec_re * ref_im, axis=1),
        ],
        axis=1,
    )
    summed = lax.psum(cross, "slab")
    corr = evaluate(summed, bins_hot, BOX)
    score = corr / math.sqrt(BOX)
    square = score * score
    weights_here = square / (4.0 + jnp.sum(square, axis=1, keepdims=True))
    mass = jnp.sum(weights_here, axis=1)
    phi_re, phi_im = steer(weights_here, bins_hot, BOX)
    tilt_hot = (work_tilt[:, None] == jnp.arange(TILTS, dtype=jnp.int32)[None, :]).astype(
        jnp.float32
    )
    wedge_flat = wedge.reshape(TILTS, planes * volume)
    wedge_rows = jnp.dot(tilt_hot, wedge_flat, precision=HIGH).reshape(rows_here, planes, volume)
    part_re = wedge_rows * (phi_re[:, None, :] * spec_re - phi_im[:, None, :] * spec_im)
    part_im = wedge_rows * (phi_re[:, None, :] * spec_im + phi_im[:, None, :] * spec_re)
    contrib = jnp.concatenate([part_re, part_im], axis=2).astype(jnp.bfloat16)
    picker = asked_local[None, :] == jnp.arange(owned, dtype=jnp.int32)[:, None]
    picker_float = picker.astype(jnp.float32)
    incoming = contrib.reshape(slots_all, planes * 2 * volume)
    volumes = (wedge_rows * mass[:, None, None]).reshape(slots_all, planes * volume)
    acc_weight = jnp.dot(picker_float, volumes, precision=HIGH)
    back = lax.all_to_all(
        weights_here.reshape(peers, capacity, ncand), "dom", split_axis=0, concat_axis=0, tiled=True
    )
    shift_weights = jnp.take(back.reshape(slots_all, ncand), slot, axis=0)
    acc_spec = jnp.dot(
        picker.astype(jnp.bfloat16), incoming, preferred_element_type=jnp.float32
    ).reshape(owned, planes, 2 * volume)
    acc_weight = acc_weight.reshape(owned, planes, volume)
    denom = acc_weight + 1.0
    fresh = jnp.concatenate(
        [acc_spec[:, :, :volume] / denom, acc_spec[:, :, volume:] / denom], axis=2
    )
    sumsq = lax.psum(jnp.sum(fresh * fresh, axis=(1, 2)), "slab")
    rms = jnp.sqrt(sumsq / (BOX * volume))
    new_refs = fresh / jnp.maximum(rms, 1.0)[:, None, None]
    return (new_refs, shift_weights)


def solution(mesh):
    placed = (
        P("dom", "slab", None),
        P("dom", "slab", None),
        P("dom"),
        P("dom", None, None),
        P("dom"),
        P(None, "slab", None),
    )
    return jax.shard_map(
        shards,
        mesh=mesh,
        in_specs=placed,
        out_specs=(P("dom", "slab", None), P("dom", None)),
        check_vma=False,
    )
```

profile of v0, /device:TPU:0, one launch (start us, length us, event | category | flops | bytes accessed | tf_op | source)
XLA Modules:
  0.0 486.5 jit_solution(16897787885077994967)
XLA Ops:
  7.2 0.8 and_select_fusion.1
  9.5 1.2 scatter_custom_fusion
  10.8 0.7 reshape.144
  12.4 1.1 gather_fusion
  13.7 0.7 reshape.216
  14.4 7.3 %all-to-all-start = ((s32[8,1,864]{2,1,0:T(1,128)}), s32[8,1,864]{2,1,0:T(1,128)S(1)}, u32[]{:S(2)}, u32[]{:S(2)}) async-start(s32[8,1,864]{2,1,0:T(1,128)} %reshape.216), calls=%async_computation | async-start | bytes 57344 | tf_op jit(solution)/shard_map/all_to_all | solution.py:97
  21.7 13.2 %gather_fusion.1 = bf16[384,8,1024]{2,1,0:T(8,128)(2,1)} fusion(bf16[192,8,1024]{2,1,0:T(8,128)(2,1)S(1)} %copy-done, s32[1024]{0:T(1024)S(1)} %pad_clamp_fusion.2), kind=kCustom, calls=%fused_computation.1 | custom fusion | bytes 12584448 | tf_op jit(solution)/shard_map/jit(_take)/gather | solution.py:89
  34.9 3.8 broadcast_select_fusion
  38.7 6.4 %copy.66 = bf16[8,48,8,1024]{3,1,2,0:T(8,128)(2,1)} copy(bf16[8,48,8,1024]{3,2,1,0:T(8,128)(2,1)S(1)} %broadcast_select_fusion) | data formatting | bytes 12582912 | tf_op jit(solution)/shard_map/jit(_take)/select_n | solution.py:89
  45.1 6.0 %all-to-all-start.1 = ((bf16[8,48,8,1024]{3,1,2,0:T(8,128)(2,1)}), bf16[8,48,8,1024]{3,1,2,0:T(8,128)(2,1)}, u32[]{:S(2)}, u32[]{:S(2)}) async-start(bf16[8,48,8,1024]{3,1,2,0:T(8,128)(2,1)} %copy.66), calls=%async_computation.1 | async-start | bytes 12582912 | tf_op jit(solution)/shard_map/all_to_all | solution.py:96
  51.2 19.0 %cosine_convert_fusion = (bf16[1024,1024]{1,0:T(8,128)(2,1)S(1)}, bf16[1024,1024]{1,0:T(8,128)(2,1)}) fusion(s32[1024]{0:T(1024)S(1)} %get-tuple-element.31, s32[1024]{0:T(1024)S(1)} %get-tuple-element.32), kind=kLoop, calls=%fused_computation.39 | loop fusion | flops 19922944 | bytes 4202496 | tf_op jit(solution)/shard_map/convert.5
  70.7 0.7 reduce.13
  71.7 14.7 %gather_fusion.2 = bf16[384,8,2048]{2,1,0:T(8,128)(2,1)} fusion(bf16[256,8,2048]{2,1,0:T(8,128)(2,1)} %param.7, s32[1024]{0:T(1024)S(1)} %pad_clamp_fusion.1), kind=kCustom, calls=%fused_computation.2 | custom fusion | bytes 25167360 | tf_op jit(solution)/shard_map/jit(_take)/gather | solution.py:102
  86.4 23.6 %copy_select_fusion = bf16[384,8,2048]{2,0,1:T(8,128)(2,1)} fusion(bf16[384,8,2048]{2,1,0:T(8,128)(2,1)} %gather_fusion.2, pred[384]{0:T(512)(128)(4,1)S(1)} %get-tuple-element.18), kind=kLoop, calls=%fused_computation.21 | loop fusion | flops 6291456 | bytes 25166208 | tf_op jit(solution)/shard_map/jit(_take)/select_n | solution.py:102
  110.0 78.8 %all-to-all-done.1 = bf16[8,48,8,1024]{3,1,2,0:T(8,128)(2,1)} async-done(((bf16[8,48,8,1024]{3,1,2,0:T(8,128)(2,1)}), bf16[8,48,8,1024]{3,1,2,0:T(8,128)(2,1)}, u32[]{:S(2)}, u32[]{:S(2)}) %all-to-all-start.1) | async-done | bytes 6291488 | tf_op jit(solution)/shard_map/all_to_all | solution.py:96
  188.8 3.7 copy.67
  192.6 18.4 %fusion.12 = f32[384,8,2048]{2,0,1:T(8,128)} fusion(bf16[384,8,1024]{2,0,1:T(8,128)(2,1)S(1)} %bitcast.130, bf16[1024,1024]{1,0:T(8,128)(2,1)} %get-tuple-element.28, bf16[1024,1024]{1,0:T(8,128)(2,1)S(1)} %get-tuple-element.27), kind=kOutput, calls=%fused_computation.35 | convolution fusion | flops 12893290496 | bytes 35651584 | tf_op jit(solution)/shard_map/dot_general | solution.py:109
  211.0 10.9 %fusion.2 = (f32[384,1024]{1,0:T(8,128)S(1)}, f32[384,1024]{1,0:T(8,128)S(1)}) fusion(f32[384,8,2048]{2,0,1:T(8,128)} %fusion.12, bf16[384,8,2048]{2,0,1:T(8,128)(2,1)S(1)} %bitcast.124), kind=kLoop, calls=%fused_computation.13 | loop fusion | flops 30670848 | bytes 40894464 | tf_op jit(solution)/shard_map/reduce_sum | solution.py:118
  221.9 2.0 pad_maximum_fusion.2
  224.2 67.4 %all-reduce.3.cloned.1.call-done = f32[384,2048]{1,0:T(8,128)} async-done(((f32[384,2048]{1,0:T(8,128)}), f32[384,2048]{1,0:T(8,128)}) %all-reduce.3.cloned.1.call-update) | async-done | bytes 3145744 | tf_op jit(solution)/shard_map/psum | solution.py:123
  291.6 3.4 fusion.139
  295.0 1.9 copy.69
  296.9 2.0 fusion.51
  298.9 1.9 fusion.60
  301.3 2.2 convolution_subtract_fusion
  303.4 2.2 convolution_add_fusion
  306.9 1.2 select_reduce_fusion.1
  308.5 2.1 select_reduce_fusion
  312.2 1.6 fusion.19
  313.8 2.8 fusion.21
  317.3 5.8 %all-to-all-start.2 = ((f32[8,1,384]{2,1,0:T(1,128)}), f32[8,1,384]{2,1,0:T(1,128)S(1)}, u32[]{:S(2)}, u32[]{:S(2)}) async-start(f32[8,1,384]{2,1,0:T(1,128)} %reshape.218), calls=%async_computation.2 | async-start | bytes 24576 | tf_op jit(solution)/shard_map/all_to_all | solution.py:143
  323.1 1.6 add_bitcast_fusion
  324.7 0.9 copy.80
  325.6 1.7 copy.81
  327.3 3.0 subtract_bitcast_fusion
  330.3 0.9 copy.76
  331.7 18.8 %multiply_convert_fusion.1 = (bf16[384,8,1024]{2,0,1:T(8,128)(2,1)S(1)}, bf16[384,8,1024]{2,0,1:T(8,128)(2,1)S(1)}, f32[384,8,1024]{2,0,1:T(8,128)}) fusion(f32[384,8,2048]{2,0,1:T(8,128)} %fusion.12, f32[384,1024]{1,0:T(8,128)} %copy.81, f32[384,1024]{1,0:T(8,128)S(1)} %copy.77, f32[384]{0:T(512)S(1)} %get-tuple-element.16, s32[384]{0:T(512)S(1)} %get-tuple-element.13, ...), kind=kOutput, calls=%fused_computation.23 | convolution fusion | flops 638588928 | bytes 54004736 | tf_op jit(solution)/shard_map/dot_general | solution.py:134
  350.5 5.2 %pad_maximum_fusion.1 = bf16[384,8,2048]{2,0,1:T(8,128)(2,1)} fusion(bf16[384,8,1024]{2,0,1:T(8,128)(2,1)S(1)} %get-tuple-element.21, bf16[384,8,1024]{2,0,1:T(8,128)(2,1)S(1)} %get-tuple-element.20), kind=kLoop, calls=%fused_computation.16 | loop fusion | flops 25165824 | bytes 25165824 | tf_op jit(solution)/shard_map/concatenate | solution.py:137
  355.7 16.6 %copy.82 = bf16[384,8,2048]{0,2,1:T(8,128)(2,1)} copy(bf16[384,8,2048]{2,0,1:T(8,128)(2,1)} %pad_maximum_fusion.1) | data formatting | bytes 25165824 | tf_op jit(solution)/shard_map/concatenate | solution.py:137
  372.3 12.6 %copy.83 = f32[384,8,1024]{0,2,1:T(8,128)} copy(f32[384,8,1024]{2,0,1:T(8,128)} %get-tuple-element.24) | data formatting | bytes 25165824 | tf_op jit(solution)/shard_map/mul | solution.py:141
  384.9 16.8 %fusion.7 = f32[256,8,2048]{2,0,1:T(8,128)} fusion(bf16[384,8,2048]{0,2,1:T(8,128)(2,1)} %copy.82, s32[384]{0:T(512)S(1)} %get-tuple-element.12), kind=kOutput, calls=%fused_computation.19 | convolution fusion | flops 3221323776 | bytes 29361664 | tf_op jit(solution)/shard_map/dot_general | solution.py:147
  401.7 35.2 %slice_divide_fusion.1 = (f32[256,8,1024]{2,0,1:T(8,128)}, f32[256,8,1024]{2,0,1:T(8,128)}) fusion(f32[256,8,2048]{2,0,1:T(8,128)} %fusion.7, f32[384,8,1024]{0,2,1:T(8,128)} %copy.83, s32[384]{0:T(512)S(1)} %get-tuple-element.12), kind=kOutput, calls=%fused_computation.25 | convolution fusion | flops 9670066176 | bytes 46138880 | tf_op jit(solution)/shard_map/dot_general | solution.py:142
  436.8 6.8 %multiply_reduce_fusion = f32[256]{0:T(256)S(1)} fusion(f32[256,8,1024]{2,0,1:T(8,128)} %get-tuple-element.23, f32[256,8,1024]{2,0,1:T(8,128)} %get-tuple-element.22), kind=kLoop, calls=%fused_computation.6 | loop fusion | flops 12582656 | bytes 16778240 | tf_op jit(solution)/shard_map/reduce_sum | solution.py:155
  443.6 5.8 %psum.15 = f32[256]{0:T(256)S(1)} all-reduce(f32[256]{0:T(256)S(1)} %multiply_reduce_fusion), channel_id=1, replica_groups=mesh['dom'=8,'slab'=4] {'slab'}, use_global_device_ids=true, to_apply=%region_10.11 | all-reduce | flops 256 | bytes 2048 | tf_op jit(solution)/shard_map/psum | solution.py:155
  449.4 7.0 %fusion = f32[256,8,2048]{2,0,1:T(8,128)S(1)} fusion(f32[256,8,1024]{2,0,1:T(8,128)} %get-tuple-element.23, f32[256,8,1024]{2,0,1:T(8,128)} %get-tuple-element.22, f32[256]{0:T(256)S(1)} %sqrt_maximum_fusion), kind=kLoop, calls=%fused_computation.11 | loop fusion | flops 8388608 | bytes 33555456 | tf_op jit(solution)/shard_map/div | solution.py:157
  456.4 20.0 %copy.86 = f32[256,8,2048]{2,1,0:T(8,128)} copy(f32[256,8,2048]{2,0,1:T(8,128)S(1)} %fusion) | data formatting | bytes 33554432
  477.0 0.7 reduce.14
  477.9 0.7 gather_fusion.3
  (75 shorter events, 9.9 us)
Async XLA Ops:
  7.2 14.5 %copy-start = (bf16[192,8,1024]{2,1,0:T(8,128)(2,1)S(1)}, bf16[192,8,1024]{2,1,0:T(8,128)(2,1)}, u32[]{:S(2)}) copy-start(bf16[192,8,1024]{2,1,0:T(8,128)(2,1)} %param.6) | copy-start | bytes 9437188
  14.4 30.8 %all-to-all-start = ((s32[8,1,864]{2,1,0:T(1,128)}), s32[8,1,864]{2,1,0:T(1,128)S(1)}, u32[]{:S(2)}, u32[]{:S(2)}) async-start(s32[8,1,864]{2,1,0:T(1,128)} %reshape.216), calls=%async_computation | async-start | bytes 57344 | tf_op jit(solution)/shard_map/all_to_all | solution.py:97
  45.1 143.7 %all-to-all-start.1 = ((bf16[8,48,8,1024]{3,1,2,0:T(8,128)(2,1)}), bf16[8,48,8,1024]{3,1,2,0:T(8,128)(2,1)}, u32[]{:S(2)}, u32[]{:S(2)}) async-start(bf16[8,48,8,1024]{3,1,2,0:T(8,128)(2,1)} %copy.66), calls=%async_computation.1 | async-start | bytes 12582912 | tf_op jit(solution)/shard_map/all_to_all | solution.py:96
  51.1 240.4 %all-reduce.3.cloned.1.call-start = ((), (), s32[]{:S(2)}) async-start(), calls=%async_computation.3 | async-start | bytes 6291456 | tf_op jit(solution)/shard_map/psum | solution.py:123
  188.8 22.2 %slice-start = ((s8[12582912]{0:T(1024)(128)(4,1)}), s8[4194304]{0:T(1024)(128)(4,1)S(1)}, s32[]{:S(2)}) async-start(s8[12582912]{0:T(1024)(128)(4,1)} %bitcast.123), calls=%async_computation.4 | async-start | bytes 8388608
  192.6 18.4 %slice-start.1 = ((s8[12582912]{0:T(1024)(128)(4,1)}), s8[4194304]{0:T(1024)(128)(4,1)S(1)}, s32[]{:S(2)}) async-start(s8[12582912]{0:T(1024)(128)(4,1)} %bitcast.123), calls=%async_computation.5 | async-start | bytes 8388608
  192.6 18.4 %slice-start.2 = ((s8[12582912]{0:T(1024)(128)(4,1)}), s8[4194304]{0:T(1024)(128)(4,1)S(1)}, s32[]{:S(2)}) async-start(s8[12582912]{0:T(1024)(128)(4,1)} %bitcast.123), calls=%async_computation.6 | async-start | bytes 8388608
  317.3 159.1 %all-to-all-start.2 = ((f32[8,1,384]{2,1,0:T(1,128)}), f32[8,1,384]{2,1,0:T(1,128)S(1)}, u32[]{:S(2)}, u32[]{:S(2)}) async-start(f32[8,1,384]{2,1,0:T(1,128)} %reshape.218), calls=%async_computation.2 | async-start | bytes 24576 | tf_op jit(solution)/shard_map/all_to_all | solution.py:143
  456.4 22.2 %copy-start.2 = (pred[192]{0:T(512)(128)(4,1)S(1)}, pred[192]{0:T(512)(128)(4,1)}, u32[]{:S(2)}) copy-start(pred[192]{0:T(512)(128)(4,1)} %get-tuple-element.14) | copy-start | bytes 580
  456.4 23.0 %copy-start.1 = (bf16[192,8,1024]{2,1,0:T(8,128)(2,1)S(1)}, bf16[192,8,1024]{2,1,0:T(8,128)(2,1)}, u32[]{:S(2)}) copy-start(bf16[192,8,1024]{2,1,0:T(8,128)(2,1)} %param.6) | copy-start | bytes 9437188
Sparse Core Ops, SparseCore 0:
  224.1 67.4 all-reduce.2
where the time goes:
time: 495 us; the launch traced here: 486 us
  waiting for transfers between devices  146 us (29%)
  matrix products  109 us (22%)
  local copies, waits for them, and re-layouts  106 us (21%)
  other arithmetic  86.2 us (17%)
  starting transfers between devices  19.1 us (4%)
  between operations  14.7 us (3%)
  blocking collectives  5.84 us (1%)
    all_to_all x1, waiting for transfers between devices, shards(): lax.all_to_all(out_rows, 'dom', split_axis=0, concat_axis=0, tiled=True)  78.8 us
    psum x1, waiting for transfers between devices, shards(): summed = lax.psum(cross, 'slab')  67.4 us
    dot_general x1, matrix products, shards(): acc_weight = jnp.dot(picker_float, volumes, precision=HIGH)  35.2 us
    select_n x2, other arithmetic, shards(): fetched = jnp.take(refs, safe, axis=0, mode='fill', fill_value=0)  23.7 us
    unnamed x20, local copies, waits for them, and re-layouts  22.5 us
    another operation x5, other arithmetic  19.7 us
    dot_general x1, matrix products, shards(): jnp.dot(tilt_hot, wedge_flat, precision=HIGH)  18.8 us
    dot_general x1, matrix products, shards(): jnp.dot(work_rows.reshape(rows_here * planes, volume), table, preferred_e...  18.4 us
  transfers between devices with their start and end apart: 4, of which 2 were waited for; matrix products, arithmetic and copies ran while one was open for 47% of the time, Pallas kernels for 0%

commit v1 on v0

--- a/solution.py
+++ b/solution.py
@@ -120,7 +120,7 @@
         ],
         axis=1,
     )
-    summed = lax.psum(cross, "slab")
+    summed = jnp.sum(lax.all_gather(cross, "slab"), axis=0)
     corr = evaluate(summed, bins_hot, BOX)
     score = corr / math.sqrt(BOX)
     square = score * score

time: 495 us -> 515 us (1.040)
  waiting for transfers between devices: 146 us -> 160 us
  other arithmetic: 86.2 us -> 92.4 us
    all_gather x0 -> x1, waiting for transfers between devices: none -> 81 us  [shards(): summed = jnp.sum(lax.all_gather(cross, 'slab'), axis=0)]
    psum x1 -> x0, waiting for transfers between devices: 67.4 us -> none  [shards(): summed = lax.psum(cross, 'slab')]
    reduce_sum x0 -> x1, other arithmetic: none -> 6.29 us  [shards(): summed = jnp.sum(lax.all_gather(cross, 'slab'), axis=0)]
    unnamed x20 -> x22, local copies, waits for them, and re-layouts: 22.5 us -> 22.5 us
  transfers between devices with their start and end apart: 4 -> 4, of which waited for: 2 -> 2; matrix products, arithmetic and copies ran while one was open for 47% -> 45% of each run, Pallas kernels for 0% -> 0%
where the time goes in v1:
time: 515 us; the launch traced here: 506 us
  waiting for transfers between devices  160 us (31%)
  matrix products  109 us (21%)
  local copies, waits for them, and re-layouts  105 us (20%)
  other arithmetic  92.4 us (18%)
  starting transfers between devices  18.9 us (4%)
  between operations  15 us (3%)
  blocking collectives  6.18 us (1%)
    all_gather x1, waiting for transfers between devices, shards(): summed = jnp.sum(lax.all_gather(cross, 'slab'), axis=0)  81 us
    all_to_all x1, waiting for transfers between devices, shards(): lax.all_to_all(out_rows, 'dom', split_axis=0, concat_axis=0, tiled=True)  79.1 us
    dot_general x1, matrix products, shards(): acc_weight = jnp.dot(picker_float, volumes, precision=HIGH)  35.2 us
    select_n x2, other arithmetic, shards(): fetched = jnp.take(refs, safe, axis=0, mode='fill', fill_value=0)  23.7 us
    unnamed x22, local copies, waits for them, and re-layouts  22.5 us
    another operation x5, other arithmetic  19.4 us
    dot_general x1, matrix products, shards(): jnp.dot(tilt_hot, wedge_flat, precision=HIGH)  18.8 us
    dot_general x1, matrix products, shards(): jnp.dot(work_rows.reshape(rows_here * planes, volume), table, preferred_e...  18.7 us
  transfers between devices with their start and end apart: 4, of which 2 were waited for; matrix products, arithmetic and copies ran while one was open for 45% of the time, Pallas kernels for 0%

profile of v1, /device:TPU:0, one launch (start us, length us, event | category | flops | bytes accessed | tf_op | source)
XLA Modules:
  0.0 505.9 jit_solution(11964167889138796416)
XLA Ops:
  7.2 0.8 and_select_fusion.1
  9.5 1.2 scatter_custom_fusion
  10.8 0.7 reshape.144
  12.4 1.1 gather_fusion
  13.7 0.7 reshape.217
  14.4 7.3 %all-to-all-start = ((s32[8,1,864]{2,1,0:T(1,128)}), s32[8,1,864]{2,1,0:T(1,128)S(1)}, u32[]{:S(2)}, u32[]{:S(2)}) async-start(s32[8,1,864]{2,1,0:T(1,128)} %reshape.217), calls=%async_computation | async-start | bytes 57344 | tf_op jit(solution)/shard_map/all_to_all | solution.py:97
  21.7 13.2 %gather_fusion.1 = bf16[384,8,1024]{2,1,0:T(8,128)(2,1)} fusion(bf16[192,8,1024]{2,1,0:T(8,128)(2,1)S(1)} %copy-done, s32[1024]{0:T(1024)S(1)} %pad_clamp_fusion.2), kind=kCustom, calls=%fused_computation.1 | custom fusion | bytes 12584448 | tf_op jit(solution)/shard_map/jit(_take)/gather | solution.py:89
  34.9 3.8 broadcast_select_fusion
  38.7 6.4 %copy.89 = bf16[8,48,8,1024]{3,1,2,0:T(8,128)(2,1)} copy(bf16[8,48,8,1024]{3,2,1,0:T(8,128)(2,1)S(1)} %broadcast_select_fusion) | data formatting | bytes 12582912 | tf_op jit(solution)/shard_map/jit(_take)/select_n | solution.py:89
  45.1 6.0 %all-to-all-start.1 = ((bf16[8,48,8,1024]{3,1,2,0:T(8,128)(2,1)}), bf16[8,48,8,1024]{3,1,2,0:T(8,128)(2,1)}, u32[]{:S(2)}, u32[]{:S(2)}) async-start(bf16[8,48,8,1024]{3,1,2,0:T(8,128)(2,1)} %copy.89), calls=%async_computation.1 | async-start | bytes 12582912 | tf_op jit(solution)/shard_map/all_to_all | solution.py:96
  51.2 18.7 %cosine_convert_fusion = (bf16[1024,1024]{1,0:T(8,128)(2,1)S(1)}, bf16[1024,1024]{1,0:T(8,128)(2,1)}) fusion(s32[1024]{0:T(1024)S(1)} %get-tuple-element.33, s32[1024]{0:T(1024)S(1)} %get-tuple-element.34), kind=kLoop, calls=%fused_computation.39 | loop fusion | flops 19922944 | bytes 4202496 | tf_op jit(solution)/shard_map/convert.5
  70.5 0.7 reduce.13
  71.4 14.7 %gather_fusion.2 = bf16[384,8,2048]{2,1,0:T(8,128)(2,1)} fusion(bf16[256,8,2048]{2,1,0:T(8,128)(2,1)} %param.7, s32[1024]{0:T(1024)S(1)} %pad_clamp_fusion.1), kind=kCustom, calls=%fused_computation.2 | custom fusion | bytes 25167360 | tf_op jit(solution)/shard_map/jit(_take)/gather | solution.py:102
  86.1 23.6 %copy_select_fusion = bf16[384,8,2048]{2,0,1:T(8,128)(2,1)} fusion(bf16[384,8,2048]{2,1,0:T(8,128)(2,1)} %gather_fusion.2, pred[384]{0:T(512)(128)(4,1)S(1)} %get-tuple-element.20), kind=kLoop, calls=%fused_computation.21 | loop fusion | flops 6291456 | bytes 25166208 | tf_op jit(solution)/shard_map/jit(_take)/select_n | solution.py:102
  109.8 79.1 %all-to-all-done.1 = bf16[8,48,8,1024]{3,1,2,0:T(8,128)(2,1)} async-done(((bf16[8,48,8,1024]{3,1,2,0:T(8,128)(2,1)}), bf16[8,48,8,1024]{3,1,2,0:T(8,128)(2,1)}, u32[]{:S(2)}, u32[]{:S(2)}) %all-to-all-start.1) | async-done | bytes 6291488 | tf_op jit(solution)/shard_map/all_to_all | solution.py:96
  188.8 3.7 copy.90
  192.6 18.7 %fusion.12 = f32[384,8,2048]{2,0,1:T(8,128)} fusion(bf16[384,8,1024]{2,0,1:T(8,128)(2,1)S(1)} %bitcast.132, bf16[1024,1024]{1,0:T(8,128)(2,1)} %get-tuple-element.30, bf16[1024,1024]{1,0:T(8,128)(2,1)S(1)} %get-tuple-element.29), kind=kOutput, calls=%fused_computation.35 | convolution fusion | flops 12893290496 | bytes 35651584 | tf_op jit(solution)/shard_map/dot_general | solution.py:109
  211.3 10.9 %fusion.2 = (f32[384,1024]{1,0:T(8,128)S(1)}, f32[384,1024]{1,0:T(8,128)S(1)}) fusion(f32[384,8,2048]{2,0,1:T(8,128)} %fusion.12, bf16[384,8,2048]{2,0,1:T(8,128)(2,1)S(1)} %bitcast.125), kind=kLoop, calls=%fused_computation.13 | loop fusion | flops 30670848 | bytes 40894464 | tf_op jit(solution)/shard_map/reduce_sum | solution.py:118
  222.2 2.0 pad_maximum_fusion.2
  224.5 81.0 %all-gather.3.cloned.1.call-done = f32[1536,2048]{1,0:T(8,128)} async-done(((f32[384,2048]{1,0:T(8,128)}), f32[1536,2048]{1,0:T(8,128)}) %all-gather.3.cloned.1.call-update) | async-done | bytes 12582928 | tf_op jit(solution)/shard_map/all_gather | solution.py:123
  305.5 6.3 %reduce_sum.66 = f32[384,2048]{1,0:T(8,128)S(1)} reduce(f32[4,384,2048]{2,1,0:T(8,128)} %bitcast.131, f32[]{:T(128)} %constant.165.clone.1), dimensions={0}, to_apply=%region_6.7 | reduce | flops 2359296 | bytes 15728644 | tf_op jit(solution)/shard_map/reduce_sum | solution.py:123
  311.8 2.2 fusion.139
  314.0 2.0 copy.92
  316.0 2.0 fusion.51
  318.0 1.9 fusion.60
  320.4 2.2 convolution_subtract_fusion
  322.5 2.2 convolution_add_fusion
  326.0 1.2 select_reduce_fusion.1
  327.6 2.3 select_reduce_fusion
  331.5 1.6 fusion.19
  333.1 2.8 fusion.21
  336.6 5.5 %all-to-all-start.2 = ((f32[8,1,384]{2,1,0:T(1,128)}), f32[8,1,384]{2,1,0:T(1,128)S(1)}, u32[]{:S(2)}, u32[]{:S(2)}) async-start(f32[8,1,384]{2,1,0:T(1,128)} %reshape.219), calls=%async_computation.2 | async-start | bytes 24576 | tf_op jit(solution)/shard_map/all_to_all | solution.py:143
  342.1 1.6 add_bitcast_fusion
  343.7 0.9 copy.103
  344.6 1.7 copy.104
  346.3 3.0 subtract_bitcast_fusion
  349.4 0.9 copy.99
  350.8 18.8 %multiply_convert_fusion.1 = (bf16[384,8,1024]{2,0,1:T(8,128)(2,1)S(1)}, bf16[384,8,1024]{2,0,1:T(8,128)(2,1)S(1)}, f32[384,8,1024]{2,0,1:T(8,128)}) fusion(f32[384,8,2048]{2,0,1:T(8,128)} %fusion.12, f32[384,1024]{1,0:T(8,128)} %copy.104, f32[384,1024]{1,0:T(8,128)S(1)} %copy.100, f32[384]{0:T(512)S(1)} %get-tuple-element.18, ...), kind=kOutput, calls=%fused_computation.23 | convolution fusion | flops 638588928 | bytes 54004736 | tf_op jit(solution)/shard_map/dot_general | solution.py:134
  369.5 5.2 %pad_maximum_fusion.1 = bf16[384,8,2048]{2,0,1:T(8,128)(2,1)} fusion(bf16[384,8,1024]{2,0,1:T(8,128)(2,1)S(1)} %get-tuple-element.23, bf16[384,8,1024]{2,0,1:T(8,128)(2,1)S(1)} %get-tuple-element.22), kind=kLoop, calls=%fused_computation.16 | loop fusion | flops 25165824 | bytes 25165824 | tf_op jit(solution)/shard_map/concatenate | solution.py:137
  374.7 16.6 %copy.105 = bf16[384,8,2048]{0,2,1:T(8,128)(2,1)} copy(bf16[384,8,2048]{2,0,1:T(8,128)(2,1)} %pad_maximum_fusion.1) | data formatting | bytes 25165824 | tf_op jit(solution)/shard_map/concatenate | solution.py:137
  391.4 12.6 %copy.106 = f32[384,8,1024]{0,2,1:T(8,128)} copy(f32[384,8,1024]{2,0,1:T(8,128)} %get-tuple-element.26) | data formatting | bytes 25165824 | tf_op jit(solution)/shard_map/mul | solution.py:141
  403.9 16.6 %fusion.7 = f32[256,8,2048]{2,0,1:T(8,128)} fusion(bf16[384,8,2048]{0,2,1:T(8,128)(2,1)} %copy.105, s32[384]{0:T(512)S(1)} %get-tuple-element.14), kind=kOutput, calls=%fused_computation.19 | convolution fusion | flops 3221323776 | bytes 29361664 | tf_op jit(solution)/shard_map/dot_general | solution.py:147
  420.5 35.2 %slice_divide_fusion.1 = (f32[256,8,1024]{2,0,1:T(8,128)}, f32[256,8,1024]{2,0,1:T(8,128)}) fusion(f32[256,8,2048]{2,0,1:T(8,128)} %fusion.7, f32[384,8,1024]{0,2,1:T(8,128)} %copy.106, s32[384]{0:T(512)S(1)} %get-tuple-element.14), kind=kOutput, calls=%fused_computation.25 | convolution fusion | flops 9670066176 | bytes 46138880 | tf_op jit(solution)/shard_map/dot_general | solution.py:142
  455.6 6.8 %multiply_reduce_fusion = f32[256]{0:T(256)S(1)} fusion(f32[256,8,1024]{2,0,1:T(8,128)} %get-tuple-element.25, f32[256,8,1024]{2,0,1:T(8,128)} %get-tuple-element.24), kind=kLoop, calls=%fused_computation.6 | loop fusion | flops 12582656 | bytes 16778240 | tf_op jit(solution)/shard_map/reduce_sum | solution.py:155
  462.4 6.2 %psum.7 = f32[256]{0:T(256)S(1)} all-reduce(f32[256]{0:T(256)S(1)} %multiply_reduce_fusion), channel_id=1, replica_groups=mesh['dom'=8,'slab'=4] {'slab'}, use_global_device_ids=true, to_apply=%region_10.11 | all-reduce | flops 256 | bytes 2048 | tf_op jit(solution)/shard_map/psum | solution.py:155
  468.6 7.0 %fusion = f32[256,8,2048]{2,0,1:T(8,128)S(1)} fusion(f32[256,8,1024]{2,0,1:T(8,128)} %get-tuple-element.25, f32[256,8,1024]{2,0,1:T(8,128)} %get-tuple-element.24, f32[256]{0:T(256)S(1)} %sqrt_maximum_fusion), kind=kLoop, calls=%fused_computation.11 | loop fusion | flops 8388608 | bytes 33555456 | tf_op jit(solution)/shard_map/div | solution.py:157
  475.6 20.0 %copy.109 = f32[256,8,2048]{2,1,0:T(8,128)} copy(f32[256,8,2048]{2,0,1:T(8,128)S(1)} %fusion) | data formatting | bytes 33554432
  496.2 0.7 reduce.14
  (78 shorter events, 10.6 us)
Async XLA Ops:
  7.2 14.5 %copy-start = (bf16[192,8,1024]{2,1,0:T(8,128)(2,1)S(1)}, bf16[192,8,1024]{2,1,0:T(8,128)(2,1)}, u32[]{:S(2)}) copy-start(bf16[192,8,1024]{2,1,0:T(8,128)(2,1)} %param.6) | copy-start | bytes 9437188
  14.4 30.8 %all-to-all-start = ((s32[8,1,864]{2,1,0:T(1,128)}), s32[8,1,864]{2,1,0:T(1,128)S(1)}, u32[]{:S(2)}, u32[]{:S(2)}) async-start(s32[8,1,864]{2,1,0:T(1,128)} %reshape.217), calls=%async_computation | async-start | bytes 57344 | tf_op jit(solution)/shard_map/all_to_all | solution.py:97
  45.1 143.7 %all-to-all-start.1 = ((bf16[8,48,8,1024]{3,1,2,0:T(8,128)(2,1)}), bf16[8,48,8,1024]{3,1,2,0:T(8,128)(2,1)}, u32[]{:S(2)}, u32[]{:S(2)}) async-start(bf16[8,48,8,1024]{3,1,2,0:T(8,128)(2,1)} %copy.89), calls=%async_computation.1 | async-start | bytes 12582912 | tf_op jit(solution)/shard_map/all_to_all | solution.py:96
  51.1 254.4 %all-gather.3.cloned.1.call-start = ((), (), s32[]{:S(2)}) async-start(), calls=%async_computation.3 | async-start | bytes 15728640 | tf_op jit(solution)/shard_map/all_gather | solution.py:123
  188.8 22.5 %slice-start = ((s8[12582912]{0:T(1024)(128)(4,1)}), s8[4194304]{0:T(1024)(128)(4,1)S(1)}, s32[]{:S(2)}) async-start(s8[12582912]{0:T(1024)(128)(4,1)} %bitcast.124), calls=%async_computation.4 | async-start | bytes 8388608
  192.6 18.7 %slice-start.1 = ((s8[12582912]{0:T(1024)(128)(4,1)}), s8[4194304]{0:T(1024)(128)(4,1)S(1)}, s32[]{:S(2)}) async-start(s8[12582912]{0:T(1024)(128)(4,1)} %bitcast.124), calls=%async_computation.5 | async-start | bytes 8388608
  192.6 18.7 %slice-start.2 = ((s8[12582912]{0:T(1024)(128)(4,1)}), s8[4194304]{0:T(1024)(128)(4,1)S(1)}, s32[]{:S(2)}) async-start(s8[12582912]{0:T(1024)(128)(4,1)} %bitcast.124), calls=%async_computation.6 | async-start | bytes 8388608
  314.0 5.9 %copy-start.2 = (f32[384,1024]{1,0:T(8,128)S(1)}, f32[384,1024]{1,0:T(8,128)}, u32[]{:S(2)}) copy-start(f32[384,1024]{1,0:T(8,128)} %get-tuple-element.27) | copy-start | bytes 4718596
  336.6 159.0 %all-to-all-start.2 = ((f32[8,1,384]{2,1,0:T(1,128)}), f32[8,1,384]{2,1,0:T(1,128)S(1)}, u32[]{:S(2)}, u32[]{:S(2)}) async-start(f32[8,1,384]{2,1,0:T(1,128)} %reshape.219), calls=%async_computation.2 | async-start | bytes 24576 | tf_op jit(solution)/shard_map/all_to_all | solution.py:143
  475.6 22.2 %copy-start.3 = (pred[192]{0:T(512)(128)(4,1)S(1)}, pred[192]{0:T(512)(128)(4,1)}, u32[]{:S(2)}) copy-start(pred[192]{0:T(512)(128)(4,1)} %get-tuple-element.16) | copy-start | bytes 580
  475.6 23.0 %copy-start.1 = (bf16[192,8,1024]{2,1,0:T(8,128)(2,1)S(1)}, bf16[192,8,1024]{2,1,0:T(8,128)(2,1)}, u32[]{:S(2)}) copy-start(bf16[192,8,1024]{2,1,0:T(8,128)(2,1)} %param.6) | copy-start | bytes 9437188
Sparse Core Ops, SparseCore 0:
  224.4 81.1 all-gather.2
